TPU v7x, 32 devices: a whole 2x2x4 slice. The times are simulated.
32 devices in a mesh: dom: 8 (over y, x, core), col: 4 (over z).
Axes of the slice: x: 2, y: 2, z: 4, core: 2. Of those that a mesh axis runs over, the one named last changes fastest.
Arguments:
- features: bfloat16 [65536, 1024], P('dom', 'col')
- weight: bfloat16 [1024, 1024], P(None, 'col'), may hold values from -0.1875 to 0.1875
- out_bias: bfloat16 [1024], P('col'), may hold values from -3 to 3
- local_index: int32 [8, 64, 4], P('dom'), may hold values from 0 to 63
- local_count: int32 [8, 64], P('dom'), may hold values from 1 to 4, as said below
- local_vals: bfloat16 [8, 64, 4, 128, 128], P('dom'), may hold values from -0.1875 to 0.1875
- halo_index: int32 [8, 64, 4], P('dom'), may hold values from 0 to 31
- halo_count: int32 [8, 64], P('dom'), may hold values from 0 to 4, as said below
- halo_vals: bfloat16 [8, 64, 4, 128, 128], P('dom'), may hold values from -0.1875 to 0.1875
- send_rows: int32 [8, 8, 512], P('dom'), may hold values from 0 to 8191
- send_count: int32 [8, 8], P('dom'), may hold values from 0 to 512, as said below
Outputs:
- normalized: bfloat16 [65536, 1024], P('dom', 'col')
- channel_stats: float32 [2, 1024], P(None, 'col')
Inputs may be any that keep to these rules, and one draw needn't show every extreme that they name: `local_index`: slots k >= local_count of a row tile are not used. `local_count`: every partition has a row tile with all 4 slots used. `halo_index`: slots k >= halo_count of a row tile are not used. `halo_count`: every partition has a row tile with all 4 slots used. `send_rows`: slots s >= send_count[q, p] are not used. send_count[p, p] is 0; every partition fills all 512 slots to some other partition.
All inputs are finite; a program needn't handle non-finite values.
Results may differ from a plain program's by a relative error of at most 0.0075.
Values may be sent and summed in bfloat16 or wider, within the bound.
A program may use at most 192 MiB of HBM per device.

v0:
```python
import jax
import jax.numpy as jnp
from jax import lax
from jax.sharding import PartitionSpec as P

TILE = 128
epsilon = 1e-06


def tile_sum(sources, tile_index, tile_count, tile_vals):
    gathered = sources[tile_index]
    keep_mask = jnp.arange(tile_vals.shape[1])[None, :] < tile_count[:, None]
    masked = jnp.where(keep_mask[:, :, None, None], tile_vals, jnp.zeros_like(tile_vals))
    return jnp.einsum("tkij,tkjc->tic", masked, gathered, preferred_element_type=jnp.float32)


def on_device(
    features,
    weight,
    out_bias,
    local_index,
    local_count,
    local_vals,
    halo_index,
    halo_count,
    halo_vals,
    send_rows,
    send_count,
):
    row_count, col_width = features.shape
    peer_count = lax.axis_size("dom")
    slot_total = send_rows.shape[2]
    chosen = features[send_rows[0]]
    keep_mask = jnp.arange(slot_total)[None, :] < send_count[0][:, None]
    outgoing = jnp.where(keep_mask[:, :, None], chosen, jnp.zeros_like(chosen))
    arrived = lax.all_to_all(outgoing, "dom", split_axis=0, concat_axis=0, tiled=True)
    halo_tiles = arrived.reshape(peer_count * slot_total // TILE, TILE, col_width)
    own_tiles = features.reshape(row_count // TILE, TILE, col_width)
    summed = tile_sum(own_tiles, local_index[0], local_count[0], local_vals[0])
    summed = summed + tile_sum(halo_tiles, halo_index[0], halo_count[0], halo_vals[0])
    spread = summed.reshape(row_count, col_width).astype(jnp.bfloat16)
    node_total = row_count * peer_count
    regrouped = lax.all_to_all(spread, "col", split_axis=0, concat_axis=1, tiled=True)
    full_weight, full_bias = (
        lax.all_gather(weight, "col", axis=1, tiled=True),
        lax.all_gather(out_bias.reshape(1, col_width), "col", axis=1, tiled=True),
    )
    mixed_rows = jnp.dot(regrouped, full_weight, preferred_element_type=jnp.float32) + full_bias[
        0
    ].astype(jnp.float32)
    active = jnp.maximum(mixed_rows, 0.0)
    row_power = jnp.mean(active * active, axis=1, keepdims=True)
    scaled = active * lax.rsqrt(row_power + epsilon)
    sum_whole, square_whole = lax.psum(
        (jnp.sum(scaled, axis=0), jnp.sum(scaled * scaled, axis=0)), ("dom", "col")
    )
    normalized = lax.all_to_all(
        scaled.astype(jnp.bfloat16), "col", split_axis=1, concat_axis=0, tiled=True
    )
    column_start = lax.axis_index("col") * col_width
    sum_total = lax.dynamic_slice_in_dim(sum_whole, column_start, col_width, 0)
    square_total = lax.dynamic_slice_in_dim(square_whole, column_start, col_width, 0)
    channel_mean = sum_total / node_total
    channel_var = square_total / node_total - channel_mean * channel_mean
    return (normalized, jnp.stack([channel_mean, channel_var]))


def solution(mesh):
    in_specs = (
        P("dom", "col"),
        P(None, "col"),
        P("col"),
        P("dom", None, None),
        P("dom", None),
        P("dom", None, None, None, None),
        P("dom", None, None),
        P("dom", None),
        P("dom", None, None, None, None),
        P("dom", None, None),
        P("dom", None),
    )
    out_specs = (P("dom", "col"), P(None, "col"))
    return jax.shard_map(
        on_device, mesh=mesh, in_specs=in_specs, out_specs=out_specs, check_vma=False
    )
```

profile of v0, /device:TPU:0, one launch (start us, length us, event | category | flops | bytes accessed | tf_op | source)
XLA Modules:
  0.0 374.6 jit_solution(2426596609186330712)
XLA Ops:
  7.2 0.7 fusion.10
  7.9 0.7 iota_compare_fusion.2
  8.6 15.7 %gather_fusion.1 = bf16[4096,256]{1,0:T(8,128)(2,1)S(1)} fusion(bf16[8192,256]{1,0:T(8,128)(2,1)} %param.11, s32[4096]{0:T(1024)S(1)} %broadcast_clamp_fusion), kind=kCustom, calls=%fused_computation.1 | custom fusion | bytes 4210688 | tf_op jit(solution)/shard_map/gather | solution.py:33
  24.4 0.0 copy-start
  24.4 0.0 copy-start.1
  24.4 1.7 broadcast_select_fusion
  26.1 5.2 %all-to-all-start = ((bf16[8,512,256]{2,1,0:T(8,128)(2,1)}), bf16[8,512,256]{2,1,0:T(8,128)(2,1)S(1)}, u32[]{:S(2)}, u32[]{:S(2)}) async-start(bf16[8,512,256]{2,1,0:T(8,128)(2,1)} %broadcast_select_fusion), calls=%async_computation | async-start | bytes 4194304 | tf_op jit(solution)/shard_map/all_to_all | solution.py:36
  31.3 0.0 copy-done
  31.3 0.1 copy.19
  31.4 0.1 reshape.208
  31.5 0.0 copy-done.1
  31.5 0.1 copy.18
  31.6 0.1 reshape.192
  31.7 0.0 copy-start.2
  31.7 0.0 copy-start.3
  31.7 12.0 %gather_fusion = bf16[256,128,256]{2,1,0:T(8,128)(2,1)} fusion(bf16[64,128,256]{2,1,0:T(8,128)(2,1)} %bitcast.52, s32[1024]{0:T(1024)S(1)} %pad_clamp_fusion.1), kind=kCustom, calls=%fused_computation | custom fusion | bytes 33555456 | tf_op jit(solution)/shard_map/gather | solution.py:11
  43.7 0.0 copy-done.2
  43.7 0.1 iota_compare_fusion
  43.8 0.0 copy-done.3
  43.8 0.1 iota_compare_fusion.1
  43.9 14.0 %all-to-all-done = bf16[8,512,256]{2,1,0:T(8,128)(2,1)S(1)} async-done(((bf16[8,512,256]{2,1,0:T(8,128)(2,1)}), bf16[8,512,256]{2,1,0:T(8,128)(2,1)S(1)}, u32[]{:S(2)}, u32[]{:S(2)}) %all-to-all-start) | async-done | bytes 2097184 | tf_op jit(solution)/shard_map/all_to_all | solution.py:36
  57.9 9.7 %gather_fusion.2 = bf16[256,128,256]{2,1,0:T(8,128)(2,1)} fusion(bf16[32,128,256]{2,1,0:T(8,128)(2,1)S(1)} %bitcast.53, s32[1024]{0:T(1024)S(1)} %pad_clamp_fusion), kind=kCustom, calls=%fused_computation.2 | custom fusion | bytes 33555456 | tf_op jit(solution)/shard_map/gather | solution.py:11
  67.6 13.8 %fusion.1 = f32[64,128,256,1]{2,1,3,0:T(8,128)} fusion(bf16[64,4,128,256]{3,2,1,0:T(8,128)(2,1)} %bitcast.54, bf16[1,64,4,128,128]{4,3,2,1,0:T(8,128)(2,1)} %param.19, pred[64,4]{1,0:T(8,128)(4,1)S(1)} %iota_compare_fusion), kind=kOutput, calls=%fused_computation.6 | convolution fusion | flops 2151677952 | bytes 33554688 | tf_op jit(solution)/shard_map/tkij,tkjc->tic/dot_general | solution.py:14
  81.4 14.0 %fusion = bf16[64,128,256]{2,1,0:T(8,128)(2,1)} fusion(f32[64,128,256,1]{2,1,3,0:T(8,128)} %fusion.1, bf16[64,4,128,256]{3,2,1,0:T(8,128)(2,1)} %bitcast.55, bf16[1,64,4,128,128]{4,3,2,1,0:T(8,128)(2,1)} %param.16, pred[64,4]{1,0:T(8,128)(4,1)S(1)} %iota_compare_fusion.1), kind=kOutput, calls=%fused_computation.4 | convolution fusion | flops 2155872256 | bytes 37748992 | tf_op jit(solution)/shard_map/tkij,tkjc->tic/dot_general | solution.py:14
  95.4 0.0 copy-start.4
  95.4 6.3 %copy.20 = bf16[4,2048,256]{1,2,0:T(8,128)(2,1)} copy(bf16[4,2048,256]{2,1,0:T(8,128)(2,1)} %bitcast.56) | data formatting | bytes 8388608 | tf_op jit(solution)/shard_map/convert_element_type | solution.py:41
  101.6 4.9 %all-to-all-start.1 = ((bf16[4,2048,256]{1,2,0:T(8,128)(2,1)}), bf16[4,2048,256]{1,2,0:T(8,128)(2,1)}, u32[]{:S(2)}, u32[]{:S(2)}) async-start(bf16[4,2048,256]{1,2,0:T(8,128)(2,1)} %copy.20), calls=%async_computation.1 | async-start | bytes 8388608 | tf_op jit(solution)/shard_map/all_to_all | solution.py:43
  106.5 0.0 all-gather.4.cloned.1.call-start
  106.5 0.7 all-gather.4.cloned.1.call-update
  107.2 0.0 copy-done.4
  107.3 103.9 %all-gather.1 = bf16[4,1,256]{2,1,0:T(2,128)(2,1)S(1)} all-gather(bf16[1,1,256]{2,1,0:T(2,128)(2,1)S(1)} %reshape.220), channel_id=2, replica_groups=mesh['dom'=8,'col'=4] {'col'}, dimensions={0}, use_global_device_ids=true | all-gather | bytes 2560 | tf_op jit(solution)/shard_map/all_gather | solution.py:46
  211.2 0.0 all-gather.4.cloned.1.call-done
  211.2 19.8 %all-to-all-done.1 = bf16[4,2048,256]{1,2,0:T(8,128)(2,1)} async-done(((bf16[4,2048,256]{1,2,0:T(8,128)(2,1)}), bf16[4,2048,256]{1,2,0:T(8,128)(2,1)}, u32[]{:S(2)}, u32[]{:S(2)}) %all-to-all-start.1) | async-done | bytes 4194336 | tf_op jit(solution)/shard_map/all_to_all | solution.py:43
  231.0 7.8 %multiply_reduce_fusion.1 = (f32[2048]{0:T(1024)S(1)}, f32[2048,1024]{0,1:T(8,128)S(1)}) fusion(f32[1024]{0:T(1024)S(1)} %bitcast.61, bf16[2048,1024]{0,1:T(8,128)(2,1)} %bitcast.19, bf16[1024,1024]{1,0:T(8,128)(2,1)} %all-gather.4.cloned.1.call-done), kind=kOutput, calls=%fused_computation.10 | convolution fusion | flops 4303353856 | bytes 14692352 | tf_op jit(solution)/shard_map/dot_general | solution.py:48
  238.8 3.5 fusion.6
  242.2 4.8 %all-to-all-start.2 = ((bf16[2048,4,256]{0,2,1:T(8,128)(2,1)}), bf16[2048,4,256]{0,2,1:T(8,128)(2,1)}, u32[]{:S(2)}, u32[]{:S(2)}) async-start(bf16[2048,4,256]{0,2,1:T(8,128)(2,1)} %bitcast.57), calls=%async_computation.2 | async-start | bytes 8388608 | tf_op jit(solution)/shard_map/all_to_all | solution.py:57
  247.1 113.8 %all-reduce = (f32[1024]{0:T(1024)S(1)}, f32[1024]{0:T(1024)S(1)}) all-reduce(f32[1024]{0:T(1024)S(1)} %get-tuple-element.3, f32[1024]{0:T(1024)S(1)} %get-tuple-element.2), channel_id=1, replica_groups=mesh['dom'=8,'col'=4] {'dom','col'}, use_global_device_ids=true, to_apply=%region_4.5 | all-reduce | flops 2048 | bytes 16384 | tf_op jit(solution)/shard_map/psum | solution.py:54
  360.9 0.1 dynamic-slice_multiply_fusion
  361.0 0.6 pad_maximum_fusion
  361.5 0.0 all-to-all-done.2
  361.6 6.2 %copy.21 = bf16[4,2048,256]{2,1,0:T(8,128)(2,1)} copy(bf16[4,2048,256]{1,2,0:T(8,128)(2,1)} %bitcast.22) | data formatting | bytes 8388608 | tf_op jit(solution)/shard_map/all_to_all | solution.py:57
  (9 shorter events, 0.1 us)
Async XLA Ops:
  24.4 6.9 %copy-start = (s32[1,64,4]{1,2,0:T(4,128)S(1)}, s32[1,64,4]{1,2,0:T(4,128)}, u32[]{:S(2)}) copy-start(s32[1,64,4]{1,2,0:T(4,128)} %param.17) | copy-start | bytes 3076
  24.4 7.1 %copy-start.1 = (s32[1,64,4]{1,2,0:T(4,128)S(1)}, s32[1,64,4]{1,2,0:T(4,128)}, u32[]{:S(2)}) copy-start(s32[1,64,4]{1,2,0:T(4,128)} %param.14) | copy-start | bytes 3076
  26.1 31.8 %all-to-all-start = ((bf16[8,512,256]{2,1,0:T(8,128)(2,1)}), bf16[8,512,256]{2,1,0:T(8,128)(2,1)S(1)}, u32[]{:S(2)}, u32[]{:S(2)}) async-start(bf16[8,512,256]{2,1,0:T(8,128)(2,1)} %broadcast_select_fusion), calls=%async_computation | async-start | bytes 4194304 | tf_op jit(solution)/shard_map/all_to_all | solution.py:36
  31.7 12.0 %copy-start.2 = (s32[1,64]{1,0:T(1,128)S(1)}, s32[1,64]{1,0:T(1,128)}, u32[]{:S(2)}) copy-start(s32[1,64]{1,0:T(1,128)} %param.18) | copy-start | bytes 772
  31.7 12.1 %copy-start.3 = (s32[1,64]{1,0:T(1,128)S(1)}, s32[1,64]{1,0:T(1,128)}, u32[]{:S(2)}) copy-start(s32[1,64]{1,0:T(1,128)} %param.15) | copy-start | bytes 772
  95.4 11.9 %copy-start.4 = (bf16[256]{0:T(256)(128)(2,1)S(1)}, bf16[256]{0:T(256)(128)(2,1)}, u32[]{:S(2)}) copy-start(bf16[256]{0:T(256)(128)(2,1)} %param.13) | copy-start | bytes 1540
  101.6 129.3 %all-to-all-start.1 = ((bf16[4,2048,256]{1,2,0:T(8,128)(2,1)}), bf16[4,2048,256]{1,2,0:T(8,128)(2,1)}, u32[]{:S(2)}, u32[]{:S(2)}) async-start(bf16[4,2048,256]{1,2,0:T(8,128)(2,1)} %copy.20), calls=%async_computation.1 | async-start | bytes 8388608 | tf_op jit(solution)/shard_map/all_to_all | solution.py:43
  106.5 104.7 %all-gather.4.cloned.1.call-start = ((), (), s32[]{:S(2)}) async-start(), calls=%async_computation.3 | async-start | bytes 2621440 | tf_op jit(solution)/shard_map/all_gather | solution.py:45
  242.2 119.3 %all-to-all-start.2 = ((bf16[2048,4,256]{0,2,1:T(8,128)(2,1)}), bf16[2048,4,256]{0,2,1:T(8,128)(2,1)}, u32[]{:S(2)}, u32[]{:S(2)}) async-start(bf16[2048,4,256]{0,2,1:T(8,128)(2,1)} %bitcast.57), calls=%async_computation.2 | async-start | bytes 8388608 | tf_op jit(solution)/shard_map/all_to_all | solution.py:57
Sparse Core Ops, SparseCore 0:
  108.9 94.7 all-gather.3
where the time goes:
time: 375 us
  blocking collectives  218 us (58%)
  local copies, waits for them, and re-layouts  50.3 us (13%)
  matrix products  35.5 us (9%)
  waiting for transfers between devices  34.5 us (9%)
  starting transfers between devices  14.9 us (4%)
  between operations  14.2 us (4%)
  other arithmetic  7.48 us (2%)
    psum x1, blocking collectives, on_device(): lax.psum((jnp.sum(scaled, axis=0), jnp.sum(scaled * scaled, axis=0)), ('d...  114 us
    all_gather x1, blocking collectives, on_device(): lax.all_gather(out_bias.reshape(1, col_width), 'col', axis=1, tiled=True)  104 us
    dot_general x2, matrix products, tile_sum(): jnp.einsum('tkij,tkjc->tic', masked, gathered, preferred_element_type=jnp...  27.7 us
    gather x2, local copies, waits for them, and re-layouts, tile_sum(): gathered = sources[tile_index]  21.7 us
    all_to_all x1, waiting for transfers between devices, on_device(): lax.all_to_all(spread, 'col', split_axis=0, concat_axis=1, tiled=True)  19.8 us
    gather x1, local copies, waits for them, and re-layouts, on_device(): chosen = features[send_rows[0]]  15.7 us
    all_to_all x1, waiting for transfers between devices, on_device(): lax.all_to_all(outgoing, 'dom', split_axis=0, concat_axis=0, tiled=True)  14 us
    dot_general x1, matrix products, on_device(): jnp.dot(regrouped, full_weight, preferred_element_type=jnp.float32)  7.76 us
  transfers between devices with their start and end apart: 4, of which 2 were waited for; matrix products, arithmetic and copies ran while one was open for 4% of the time, Pallas kernels for 0%

commit v1 on v0

--- a/solution.py
+++ b/solution.py
@@ -5,6 +5,18 @@
 
 TILE = 128
 epsilon = 1e-06
+
+
+def gather_by_bits(x, axis, dim):
+    ways, here, step = (lax.axis_size(axis), lax.axis_index(axis), x.shape[dim])
+    line, have = (x, 1)
+    while have < ways:
+        line = jnp.concatenate(
+            [line, lax.ppermute(line, axis, [(d, (d - have) % ways) for d in range(ways)])],
+            axis=dim,
+        )
+        have = 2 * have
+    return jnp.roll(line, here * step, axis=dim)
 
 
 def tile_sum(sources, tile_index, tile_count, tile_vals):
@@ -43,7 +55,7 @@
     regrouped = lax.all_to_all(spread, "col", split_axis=0, concat_axis=1, tiled=True)
     full_weight, full_bias = (
         lax.all_gather(weight, "col", axis=1, tiled=True),
-        lax.all_gather(out_bias.reshape(1, col_width), "col", axis=1, tiled=True),
+        gather_by_bits(out_bias.reshape(1, col_width), "col", 1),
     )
     mixed_rows = jnp.dot(regrouped, full_weight, preferred_element_type=jnp.float32) + full_bias[
         0

time: 375 us -> 377 us (level)
  blocking collectives: 218 us -> 114 us
  waiting for transfers between devices: 34.5 us -> 110 us
  starting transfers between devices: 14.9 us -> 44.3 us
    all_gather x1 -> x0, blocking collectives: 104 us -> none  [on_device(): lax.all_gather(out_bias.reshape(1, col_width), 'col', axis=1, tiled=True)]
    ppermute x0 -> x2, waiting for transfers between devices: none -> 95.7 us  [gather_by_bits(): lax.ppermute(line, axis, [(d, (d - have) % ways) for d in range(ways)])]
    ppermute x0 -> x2, starting transfers between devices: none -> 29.1 us  [gather_by_bits(): lax.ppermute(line, axis, [(d, (d - have) % ways) for d in range(ways)])]
    all_to_all x1, waiting for transfers between devices: 19.8 us -> 0.01 us  [on_device(): lax.all_to_all(spread, 'col', split_axis=0, concat_axis=1, tiled=True)]
  transfers between devices with their start and end apart: 4 -> 6, of which waited for: 2 -> 3; matrix products, arithmetic and copies ran while one was open for 4% -> 4% of each run, Pallas kernels for 0% -> 0%
where the time goes in v1:
time: 377 us; the launch traced here: 376 us
  blocking collectives  114 us (30%)
  waiting for transfers between devices  110 us (29%)
  local copies, waits for them, and re-layouts  50.4 us (13%)
  starting transfers between devices  44.3 us (12%)
  matrix products  35.5 us (9%)
  between operations  14.2 us (4%)
  other arithmetic  7.49 us (2%)
    psum x1, blocking collectives, on_device(): lax.psum((jnp.sum(scaled, axis=0), jnp.sum(scaled * scaled, axis=0)), ('d...  114 us
    ppermute x2, waiting for transfers between devices, gather_by_bits(): lax.ppermute(line, axis, [(d, (d - have) % ways) for d in range(ways)])  95.7 us
    ppermute x2, starting transfers between devices, gather_by_bits(): lax.ppermute(line, axis, [(d, (d - have) % ways) for d in range(ways)])  29.1 us
    dot_general x2, matrix products, tile_sum(): jnp.einsum('tkij,tkjc->tic', masked, gathered, preferred_element_type=jnp...  27.7 us
    gather x2, local copies, waits for them, and re-layouts, tile_sum(): gathered = sources[tile_index]  21.7 us
    gather x1, local copies, waits for them, and re-layouts, on_device(): chosen = features[send_rows[0]]  15.7 us
    all_to_all x1, waiting for transfers between devices, on_device(): lax.all_to_all(outgoing, 'dom', split_axis=0, concat_axis=0, tiled=True)  14 us
    dot_general x1, matrix products, on_device(): jnp.dot(regrouped, full_weight, preferred_element_type=jnp.float32)  7.77 us
  transfers between devices with their start and end apart: 6, of which 3 were waited for; matrix products, arithmetic and copies ran while one was open for 4% of the time, Pallas kernels for 0%

profile of v1, /device:TPU:0, one launch (start us, length us, event | category | flops | bytes accessed | tf_op | source)
XLA Modules:
  0.0 376.4 jit_solution(2648290293444759671)
XLA Ops:
  7.2 0.7 fusion.10
  7.9 0.7 iota_compare_fusion.2
  8.6 15.7 %gather_fusion.1 = bf16[4096,256]{1,0:T(8,128)(2,1)S(1)} fusion(bf16[8192,256]{1,0:T(8,128)(2,1)} %param.11, s32[4096]{0:T(1024)S(1)} %broadcast_clamp_fusion), kind=kCustom, calls=%fused_computation.1 | custom fusion | bytes 4210688 | tf_op jit(solution)/shard_map/gather | solution.py:45
  24.4 0.0 copy-start
  24.4 0.0 copy-start.1
  24.4 1.7 broadcast_select_fusion
  26.1 5.2 %all-to-all-start = ((bf16[8,512,256]{2,1,0:T(8,128)(2,1)}), bf16[8,512,256]{2,1,0:T(8,128)(2,1)S(1)}, u32[]{:S(2)}, u32[]{:S(2)}) async-start(bf16[8,512,256]{2,1,0:T(8,128)(2,1)} %broadcast_select_fusion), calls=%async_computation | async-start | bytes 4194304 | tf_op jit(solution)/shard_map/all_to_all | solution.py:48
  31.3 0.0 copy-done
  31.3 0.1 copy.15
  31.4 0.1 reshape.208
  31.5 0.0 copy-done.1
  31.5 0.1 copy.14
  31.6 0.1 reshape.192
  31.7 0.0 copy-start.2
  31.7 0.0 copy-start.3
  31.7 12.0 %gather_fusion = bf16[256,128,256]{2,1,0:T(8,128)(2,1)} fusion(bf16[64,128,256]{2,1,0:T(8,128)(2,1)} %bitcast.52, s32[1024]{0:T(1024)S(1)} %pad_clamp_fusion.1), kind=kCustom, calls=%fused_computation | custom fusion | bytes 33555456 | tf_op jit(solution)/shard_map/gather | solution.py:23
  43.7 0.0 copy-done.2
  43.7 0.1 iota_compare_fusion
  43.8 0.0 copy-done.3
  43.8 0.1 iota_compare_fusion.1
  43.9 14.0 %all-to-all-done = bf16[8,512,256]{2,1,0:T(8,128)(2,1)S(1)} async-done(((bf16[8,512,256]{2,1,0:T(8,128)(2,1)}), bf16[8,512,256]{2,1,0:T(8,128)(2,1)S(1)}, u32[]{:S(2)}, u32[]{:S(2)}) %all-to-all-start) | async-done | bytes 2097184 | tf_op jit(solution)/shard_map/all_to_all | solution.py:48
  57.9 9.7 %gather_fusion.2 = bf16[256,128,256]{2,1,0:T(8,128)(2,1)} fusion(bf16[32,128,256]{2,1,0:T(8,128)(2,1)S(1)} %bitcast.53, s32[1024]{0:T(1024)S(1)} %pad_clamp_fusion), kind=kCustom, calls=%fused_computation.2 | custom fusion | bytes 33555456 | tf_op jit(solution)/shard_map/gather | solution.py:23
  67.6 13.8 %fusion.1 = f32[64,128,256,1]{2,1,3,0:T(8,128)} fusion(bf16[64,4,128,256]{3,2,1,0:T(8,128)(2,1)} %bitcast.54, bf16[1,64,4,128,128]{4,3,2,1,0:T(8,128)(2,1)} %param.19, pred[64,4]{1,0:T(8,128)(4,1)S(1)} %iota_compare_fusion), kind=kOutput, calls=%fused_computation.6 | convolution fusion | flops 2151677952 | bytes 33554688 | tf_op jit(solution)/shard_map/tkij,tkjc->tic/dot_general | solution.py:26
  81.4 14.0 %fusion = bf16[64,128,256]{2,1,0:T(8,128)(2,1)} fusion(f32[64,128,256,1]{2,1,3,0:T(8,128)} %fusion.1, bf16[64,4,128,256]{3,2,1,0:T(8,128)(2,1)} %bitcast.55, bf16[1,64,4,128,128]{4,3,2,1,0:T(8,128)(2,1)} %param.16, pred[64,4]{1,0:T(8,128)(4,1)S(1)} %iota_compare_fusion.1), kind=kOutput, calls=%fused_computation.4 | convolution fusion | flops 2155872256 | bytes 37748992 | tf_op jit(solution)/shard_map/tkij,tkjc->tic/dot_general | solution.py:26
  95.4 0.0 copy-start.4
  95.4 6.3 %copy.16 = bf16[4,2048,256]{1,2,0:T(8,128)(2,1)} copy(bf16[4,2048,256]{2,1,0:T(8,128)(2,1)} %bitcast.56) | data formatting | bytes 8388608 | tf_op jit(solution)/shard_map/convert_element_type | solution.py:53
  101.6 4.9 %all-to-all-start.1 = ((bf16[4,2048,256]{1,2,0:T(8,128)(2,1)}), bf16[4,2048,256]{1,2,0:T(8,128)(2,1)}, u32[]{:S(2)}, u32[]{:S(2)}) async-start(bf16[4,2048,256]{1,2,0:T(8,128)(2,1)} %copy.16), calls=%async_computation.1 | async-start | bytes 8388608 | tf_op jit(solution)/shard_map/all_to_all | solution.py:55
  106.5 0.0 all-gather.2.cloned.1.call-start
  106.5 0.7 all-gather.2.cloned.1.call-update
  107.2 0.0 copy-done.4
  107.2 4.1 %collective-permute-start = (bf16[1,256]{1,0:T(2,128)(2,1)S(1)}, bf16[1,256]{1,0:T(2,128)(2,1)S(1)}, u32[]{:S(2)}, u32[]{:S(2)}) collective-permute-start(bf16[1,256]{1,0:T(2,128)(2,1)S(1)} %reshape.188), channel_id=1, source_target_pairs={{0,3},{1,0},{2,1},{3,2},{4,7},{5,4},{6,5},{7,6},{8,11},{9,8},{10,9... | collective-permute-start | bytes 1544 | tf_op jit(solution)/shard_map/ppermute | solution.py:15
  111.3 94.1 %collective-permute-done = bf16[1,256]{1,0:T(2,128)(2,1)S(1)} collective-permute-done((bf16[1,256]{1,0:T(2,128)(2,1)S(1)}, bf16[1,256]{1,0:T(2,128)(2,1)S(1)}, u32[]{:S(2)}, u32[]{:S(2)}) %collective-permute-start) | collective-permute-done | bytes 544 | tf_op jit(solution)/shard_map/ppermute | solution.py:15
  205.4 25.1 %collective-permute-start.1 = (bf16[1,512]{1,0:T(2,128)(2,1)S(1)}, bf16[1,512]{1,0:T(2,128)(2,1)S(1)}, u32[]{:S(2)}, u32[]{:S(2)}) collective-permute-start(bf16[1,512]{1,0:T(2,128)(2,1)S(1)} %pad_maximum_fusion), channel_id=1, source_target_pairs={{0,2},{1,3},{2,0},{3,1},{4,6},{5,7},{6,4},{7,5},{8,10},{9,11},{10,... | collective-permute-start | bytes 3080 | tf_op jit(solution)/shard_map/ppermute | solution.py:15
  230.5 1.6 collective-permute-done.1
  232.1 0.0 all-gather.2.cloned.1.call-done
  232.1 0.0 all-to-all-done.1
  232.1 7.8 %multiply_reduce_fusion.1 = (f32[2048]{0:T(1024)S(1)}, f32[2048,1024]{0,1:T(8,128)S(1)}) fusion(f32[1024]{0:T(1024)S(1)} %bitcast.61, bf16[2048,1024]{0,1:T(8,128)(2,1)} %bitcast.19, bf16[1024,1024]{1,0:T(8,128)(2,1)} %all-gather.2.cloned.1.call-done), kind=kOutput, calls=%fused_computation.10 | convolution fusion | flops 4303353856 | bytes 14692352 | tf_op jit(solution)/shard_map/dot_general | solution.py:60
  239.9 3.5 fusion.6
  243.4 5.1 %all-to-all-start.2 = ((bf16[2048,4,256]{0,2,1:T(8,128)(2,1)}), bf16[2048,4,256]{0,2,1:T(8,128)(2,1)}, u32[]{:S(2)}, u32[]{:S(2)}) async-start(bf16[2048,4,256]{0,2,1:T(8,128)(2,1)} %bitcast.57), calls=%async_computation.2 | async-start | bytes 8388608 | tf_op jit(solution)/shard_map/all_to_all | solution.py:69
  248.5 114.2 %all-reduce = (f32[1024]{0:T(1024)S(1)}, f32[1024]{0:T(1024)S(1)}) all-reduce(f32[1024]{0:T(1024)S(1)} %get-tuple-element.3, f32[1024]{0:T(1024)S(1)} %get-tuple-element.2), channel_id=1, replica_groups=mesh['dom'=8,'col'=4] {'dom','col'}, use_global_device_ids=true, to_apply=%region_4.5 | all-reduce | flops 2048 | bytes 16384 | tf_op jit(solution)/shard_map/psum | solution.py:66
  362.7 0.1 dynamic-slice_multiply_fusion
  362.8 0.6 pad_maximum_fusion.1
  363.4 0.0 all-to-all-done.2
  363.4 6.2 %copy.17 = bf16[4,2048,256]{2,1,0:T(8,128)(2,1)} copy(bf16[4,2048,256]{1,2,0:T(8,128)(2,1)} %bitcast.22) | data formatting | bytes 8388608 | tf_op jit(solution)/shard_map/all_to_all | solution.py:69
  (16 shorter events, 0.1 us)
Async XLA Ops:
  24.4 6.9 %copy-start = (s32[1,64,4]{1,2,0:T(4,128)S(1)}, s32[1,64,4]{1,2,0:T(4,128)}, u32[]{:S(2)}) copy-start(s32[1,64,4]{1,2,0:T(4,128)} %param.17) | copy-start | bytes 3076
  24.4 7.1 %copy-start.1 = (s32[1,64,4]{1,2,0:T(4,128)S(1)}, s32[1,64,4]{1,2,0:T(4,128)}, u32[]{:S(2)}) copy-start(s32[1,64,4]{1,2,0:T(4,128)} %param.14) | copy-start | bytes 3076
  26.1 31.8 %all-to-all-start = ((bf16[8,512,256]{2,1,0:T(8,128)(2,1)}), bf16[8,512,256]{2,1,0:T(8,128)(2,1)S(1)}, u32[]{:S(2)}, u32[]{:S(2)}) async-start(bf16[8,512,256]{2,1,0:T(8,128)(2,1)} %broadcast_select_fusion), calls=%async_computation | async-start | bytes 4194304 | tf_op jit(solution)/shard_map/all_to_all | solution.py:48
  31.7 12.0 %copy-start.2 = (s32[1,64]{1,0:T(1,128)S(1)}, s32[1,64]{1,0:T(1,128)}, u32[]{:S(2)}) copy-start(s32[1,64]{1,0:T(1,128)} %param.18) | copy-start | bytes 772
  31.7 12.1 %copy-start.3 = (s32[1,64]{1,0:T(1,128)S(1)}, s32[1,64]{1,0:T(1,128)}, u32[]{:S(2)}) copy-start(s32[1,64]{1,0:T(1,128)} %param.15) | copy-start | bytes 772
  95.4 11.9 %copy-start.4 = (bf16[256]{0:T(256)(128)(2,1)S(1)}, bf16[256]{0:T(256)(128)(2,1)}, u32[]{:S(2)}) copy-start(bf16[256]{0:T(256)(128)(2,1)} %param.13) | copy-start | bytes 1540
  101.6 130.5 %all-to-all-start.1 = ((bf16[4,2048,256]{1,2,0:T(8,128)(2,1)}), bf16[4,2048,256]{1,2,0:T(8,128)(2,1)}, u32[]{:S(2)}, u32[]{:S(2)}) async-start(bf16[4,2048,256]{1,2,0:T(8,128)(2,1)} %copy.16), calls=%async_computation.1 | async-start | bytes 8388608 | tf_op jit(solution)/shard_map/all_to_all | solution.py:55
  106.5 125.6 %all-gather.2.cloned.1.call-start = ((), (), s32[]{:S(2)}) async-start(), calls=%async_computation.3 | async-start | bytes 2621440 | tf_op jit(solution)/shard_map/all_gather | solution.py:57
  107.2 98.2 %collective-permute-start = (bf16[1,256]{1,0:T(2,128)(2,1)S(1)}, bf16[1,256]{1,0:T(2,128)(2,1)S(1)}, u32[]{:S(2)}, u32[]{:S(2)}) collective-permute-start(bf16[1,256]{1,0:T(2,128)(2,1)S(1)} %reshape.188), channel_id=1, source_target_pairs={{0,3},{1,0},{2,1},{3,2},{4,7},{5,4},{6,5},{7,6},{8,11},{9,8},{10,9... | collective-permute-start | bytes 1544 | tf_op jit(solution)/shard_map/ppermute | solution.py:15
  205.4 26.6 %collective-permute-start.1 = (bf16[1,512]{1,0:T(2,128)(2,1)S(1)}, bf16[1,512]{1,0:T(2,128)(2,1)S(1)}, u32[]{:S(2)}, u32[]{:S(2)}) collective-permute-start(bf16[1,512]{1,0:T(2,128)(2,1)S(1)} %pad_maximum_fusion), channel_id=1, source_target_pairs={{0,2},{1,3},{2,0},{3,1},{4,6},{5,7},{6,4},{7,5},{8,10},{9,11},{10,... | collective-permute-start | bytes 3080 | tf_op jit(solution)/shard_map/ppermute | solution.py:15
  243.4 120.0 %all-to-all-start.2 = ((bf16[2048,4,256]{0,2,1:T(8,128)(2,1)}), bf16[2048,4,256]{0,2,1:T(8,128)(2,1)}, u32[]{:S(2)}, u32[]{:S(2)}) async-start(bf16[2048,4,256]{0,2,1:T(8,128)(2,1)} %bitcast.57), calls=%async_computation.2 | async-start | bytes 8388608 | tf_op jit(solution)/shard_map/all_to_all | solution.py:69
Sparse Core Ops, SparseCore 0:
  108.9 94.7 all-gather.1
